TPU v7x, 32 devices: a whole 2x2x4 slice. The times are simulated.
32 devices in a mesh: seq: 16 (over z, y, x), dp: 2 (over core).
Axes of the slice: x: 2, y: 2, z: 4, core: 2. Of those that a mesh axis runs over, the one named last changes fastest.
Arguments:
- block_pos: int32 [2, 32], P('dp'), may hold values from 0 to 31, as said below
- queries: bfloat16 [2, 2048, 2048], P('dp', 'seq'), may hold values from -8 to 8
- keys: bfloat16 [2, 2048, 2048], P('dp', 'seq'), may hold values from -4 to 4
- values: bfloat16 [2, 2048, 2048], P('dp', 'seq'), may hold values from -4 to 4
- attn_out: bfloat16 [2, 2048, 2048], P('dp', 'seq'), may hold values from -4 to 4, as said below
- log_sums: float32 [2, 16, 2048], P('dp', None, 'seq'), as said below
- grad_out: bfloat16 [2, 2048, 2048], P('dp', 'seq'), may hold values from -0.375 to 0.375
- out_weight: bfloat16 [2048, 2048], replicated, may hold values from -12 to 12
Outputs:
- grad_queries: bfloat16 [2, 2048, 2048], P('dp', 'seq')
- grad_keys: bfloat16 [2, 2048, 2048], P('dp', 'seq')
- grad_values: bfloat16 [2, 2048, 2048], P('dp', 'seq')
- grad_weight: float32 [2048, 2048], P('seq')
Inputs may be any that keep to these rules, and one draw needn't show every extreme that they name: Each row is a permutation of 0 to 31; row block c (rows c * 64 to c * 64 + 63) holds the rows at positions block_pos[b, c] * 64 onward, in order. attn_out is the forward attention output: per head, exp(scores - log_sums) on the allowed keys times values, rounded to bfloat16. log_sums[b, h, t] is the log of the sum of exp(scores[b, h, t, u]) over the keys u with pos[b, u] <= pos[b, t].
All inputs are finite; a program needn't handle non-finite values.
Results may differ from a plain program's by a relative error of at most 0.0075.
Values may be sent and summed in bfloat16 or wider, within the bound.
A program may use at most 320 MiB of HBM per device.

v0:
```python
import functools

import jax
import jax.numpy as jnp
from jax import lax
from jax.experimental import pallas as pl
from jax.experimental.pallas import tpu as pltpu
from jax.sharding import PartitionSpec as P


def shifted(shard, axis, by):
    count = lax.axis_size(axis)
    return lax.ppermute(shard, axis, [(i, (i + by) % count) for i in range(count)])


def slot_positions(table_row, owners, half_rows):
    slot_ids = owners[:, None] * 2 + jnp.arange(2, dtype=jnp.int32)[None, :]
    pick_rows = (
        slot_ids[:, :, None] == jnp.arange(table_row.shape[0], dtype=jnp.int32)[None, None, :]
    ).astype(jnp.int32)
    block_ids = jnp.sum(pick_rows * table_row[None, None, :], axis=-1)
    offsets = jnp.arange(half_rows, dtype=jnp.int32)
    return (block_ids[:, :, None] * half_rows + offsets[None, None, :]).reshape(
        owners.shape[0], 2 * half_rows
    )


def block_core(
    query_rows, grad_rows, log_block, delta_block, key_rows, value_rows, allowed, scaling
):
    head_count = log_block.shape[0]
    query_len = query_rows.shape[0]
    key_len = key_rows.shape[0]
    query_heads = query_rows.reshape(query_len, head_count, -1)
    grad_split = grad_rows.reshape(query_len, head_count, -1)
    key_heads = key_rows.reshape(key_len, head_count, -1)
    value_heads = value_rows.reshape(key_len, head_count, -1)
    scores = (
        jnp.einsum("ahd,bhd->hab", query_heads, key_heads, preferred_element_type=jnp.float32)
        * scaling
    )
    attn_probs = jnp.where(allowed[None], jnp.exp(scores - log_block[:, :, None]), 0.0)
    probs_low = attn_probs.astype(jnp.bfloat16)
    dprobs = jnp.einsum("ahd,bhd->hab", grad_split, value_heads, preferred_element_type=jnp.float32)
    dscores = attn_probs * (dprobs - delta_block[:, :, None])
    dscores_low = dscores.astype(jnp.bfloat16)
    value_part = jnp.einsum(
        "hab,ahd->bhd", probs_low, grad_split, preferred_element_type=jnp.float32
    )
    key_part = (
        jnp.einsum("hab,ahd->bhd", dscores_low, query_heads, preferred_element_type=jnp.float32)
        * scaling
    )
    query_part = (
        jnp.einsum("hab,bhd->ahd", dscores_low, key_heads, preferred_element_type=jnp.float32)
        * scaling
    )
    return (
        query_part.reshape(query_len, -1),
        key_part.reshape(key_len, -1),
        value_part.reshape(key_len, -1),
    )


def block_grads(
    query_rows, grad_rows, log_block, delta_block, key_rows, value_rows, allowed, scaling
):
    parts = block_core(
        query_rows, grad_rows, log_block, delta_block, key_rows, value_rows, allowed, scaling
    )
    return (parts[0], parts[1].astype(jnp.bfloat16), parts[2].astype(jnp.bfloat16))


def grid_per_device(block_pos, queries, keys, values, attn_out, log_sums, grad_out, out_weight):
    dev_count = lax.axis_size("seq")
    grid_side = 4 + 4 * (dev_count // 64)
    my_index = lax.axis_index("seq")
    table_row = block_pos[0]
    own_queries = queries[0]
    tok_rows = own_queries.shape[0]
    half_rows = tok_rows // 2
    head_count = log_sums.shape[1]
    width_all = own_queries.shape[1]
    scaling = (width_all // head_count) ** (-0.5)
    cotangent = grad_out[0]
    grad_heads = lax.dot_general(
        cotangent, out_weight, (((1,), (1,)), ((), ())), preferred_element_type=jnp.float32
    ).astype(jnp.bfloat16)
    deltas = jnp.einsum(
        "ahd,ahd->ha",
        grad_heads.reshape(tok_rows, head_count, -1),
        attn_out[0].reshape(tok_rows, head_count, -1),
        preferred_element_type=jnp.float32,
    )
    query_pack = (own_queries[None], grad_heads[None], log_sums[0][None], deltas[None])
    key_pack = (keys[0][None], values[0][None])
    query_list = [query_pack]
    key_list = [key_pack]
    for offset in range(1, grid_side):
        query_list.append(
            (
                shifted(query_pack[0].astype(jnp.float32), "seq", offset).astype(jnp.bfloat16),
                shifted(query_pack[1].astype(jnp.float32), "seq", offset).astype(jnp.bfloat16),
                shifted(query_pack[2], "seq", offset),
                shifted(query_pack[3], "seq", offset),
            )
        )
        key_list.append(shifted((key_pack[0], key_pack[1]), "seq", offset * grid_side))
    query_stack = tuple(
        (jnp.concatenate([parcel[member] for parcel in query_list], axis=0) for member in range(4))
    )
    key_stack = tuple(
        (jnp.concatenate([parcel[member] for parcel in key_list], axis=0) for member in range(2))
    )
    query_rows = query_stack[0].reshape(-1, width_all)
    grad_rows = query_stack[1].reshape(-1, width_all)
    log_block = jnp.transpose(query_stack[2], (1, 0, 2)).reshape(head_count, -1)
    delta_block = jnp.transpose(query_stack[3], (1, 0, 2)).reshape(head_count, -1)
    query_owners = (my_index - jnp.arange(grid_side, dtype=jnp.int32)) % dev_count
    key_owners = (my_index - jnp.arange(grid_side, dtype=jnp.int32) * grid_side) % dev_count
    query_pos = slot_positions(table_row, query_owners, half_rows).reshape(-1)
    key_pos = slot_positions(table_row, key_owners, half_rows)
    query_total = jnp.zeros((grid_side * tok_rows, width_all), jnp.float32)
    key_results = []
    for offset in range(grid_side):
        key_now = key_stack[0][offset]
        value_now = key_stack[1][offset]
        allowed = key_pos[offset][None, :] <= query_pos[:, None]
        results = block_grads(
            query_rows, grad_rows, log_block, delta_block, key_now, value_now, allowed, scaling
        )
        query_total = query_total + results[0]
        key_results.append((results[1], results[2]))
    query_parts = query_total.astype(jnp.bfloat16).reshape(grid_side, tok_rows, width_all)
    query_sum = query_parts[0].astype(jnp.float32)
    for offset in range(1, grid_side):
        query_sum = query_sum + shifted(query_parts[offset], "seq", -offset).astype(jnp.float32)
    key_sum = key_results[0][0].astype(jnp.float32)
    value_sum = key_results[0][1].astype(jnp.float32)
    for offset in range(1, grid_side):
        returned = shifted(
            (key_results[offset][0], key_results[offset][1]), "seq", -offset * grid_side
        )
        key_sum = key_sum + returned[0].astype(jnp.float32)
        value_sum = value_sum + returned[1].astype(jnp.float32)
    columns = attn_out[0]
    weight_share = lax.psum_scatter(
        lax.dot_general(
            columns, cotangent, (((0,), (0,)), ((), ())), preferred_element_type=jnp.float32
        ),
        ("seq", "dp"),
        scatter_dimension=0,
        tiled=True,
    )
    weight_share = lax.all_gather(
        weight_share.astype(jnp.bfloat16), "dp", axis=0, tiled=True
    ).astype(weight_share.dtype)
    return (
        query_sum.astype(jnp.bfloat16)[None],
        key_sum.astype(jnp.bfloat16)[None],
        value_sum.astype(jnp.bfloat16)[None],
        weight_share,
    )


MESH = pl.DeviceIdType.MESH
ANY = pl.BlockSpec(memory_space=pl.ANY)


def enter(count, cores, me, core):
    barrier = pltpu.get_barrier_semaphore()
    for step in range(1, count):
        pl.semaphore_signal(
            barrier, inc=1, device_id=(lax.rem(me + step, count), core), device_id_type=MESH
        )
    total = count - 1
    for turn in range(1, cores):
        peer = (me, lax.rem(core + turn, cores))
        pl.semaphore_signal(barrier, inc=1, device_id=peer, device_id_type=MESH)
        total += 1
    pl.semaphore_wait(barrier, total)


def fused_kernel(
    count, side, cores, dim, tile, scaling,
    sources, places, q_in, k_in, v_in, a_in, b_in, l_in, w_in,
    q_out, k_out, v_out, w_out,
    q_all, k_all, v_all, g_all, s_all, a_all, b_all,
    a_own, b_own, l_own, w_own, g_own, s_own,
    q_row, k_row, v_row, g_row, s_row, dq, dk, dv,
    q_back, k_back, v_back, w_part, w_line, w_half, w_core, w_land,
    send, recv, plane_send, plane_recv, line_send, line_recv,
    back_send, back_recv, half_send, half_recv, core_send, core_recv, local,
):
    me = lax.axis_index("seq")
    core = lax.axis_index("dp")
    column = lax.rem(me, side)
    plane = me - column
    row = me // side
    half = w_half.shape[2]
    groups, _, _, _, sub = w_core.shape
    low = jnp.bfloat16

    loads = [
        pltpu.make_async_copy(source, target, local.at[at])
        for at, (source, target) in enumerate(
            [(b_in, b_own), (w_in, w_own), (a_in, a_own), (l_in, l_own)]
        )
    ]
    for copy in loads:
        copy.start()
    enter(count, cores, me, core)

    def head_cut(head):
        return pl.ds(pl.multiple_of(head * dim, dim), dim)

    rows = a_all.shape[1]

    def owner_blocks(owner):
        return pl.ds(owner * 2, 2)

    def remote(source, target, sender, receiver, device):
        return pltpu.make_async_remote_copy(
            source, target, sender, receiver, device_id=device, device_id_type=MESH
        )

    def row_pieces(head, owner):
        cut = head_cut(head)
        return [
            (q_in.at[:, :, cut], q_all.at[owner_blocks(owner)]),
            (k_in.at[:, :, cut], k_all.at[owner_blocks(owner)]),
            (v_in.at[:, :, cut], v_all.at[owner_blocks(owner)]),
        ]

    def grad_pieces(head, owner):
        return [
            (g_own.at[head], g_all.at[owner_blocks(owner)]),
            (s_own.at[head], s_all.at[owner_blocks(owner)]),
        ]

    def head_copies(pieces, base, out_index, in_index, device):
        return [
            remote(source, target, send.at[base + at, out_index], recv.at[base + at, in_index], device)
            for at, (source, target) in enumerate(pieces)
        ]

    def plane_pieces(to_column, slot):
        pairs = []
        for part in range(side):
            cut = head_cut(part * side + to_column)
            pairs.append((a_in.at[:, cut], a_all.at[slot, :, pl.ds(part * dim, dim)]))
        for group in range(groups):
            for to_core in range(cores):
                cut = pl.ds(to_core * half + group * sub, sub)
                pairs.append((b_in.at[:, cut], b_all.at[slot, :, cut]))
        return pairs

    def group_of(copies, group):
        first = side + group * cores if group else 0
        return copies[first : side + (group + 1) * cores]

    def plane_copies(to_column, slot, out_index, in_index, device):
        return [
            remote(source, target, plane_send.at[at, out_index], plane_recv.at[at, in_index], device)
            for at, (source, target) in enumerate(plane_pieces(to_column, slot))
        ]

    def plane_peer(step):
        return lax.rem(column + step, side)

    def far_first(turn):
        far = count - side
        return jnp.where(turn < far, turn + side, lax.rem(turn - far + 1, side))

    def core_copy(group, to_core, slot, turn):
        return remote(
            w_core.at[group, to_core], w_land.at[group, slot], core_send.at[group, turn],
            core_recv.at[group, slot], (me, to_core),
        )

    def line_copy(group, to_row, slot, out_index, in_index, device):
        return remote(
            w_part.at[group, to_row], w_line.at[group, slot], line_send.at[group, out_index],
            line_recv.at[group, in_index], device,
        )

    def back_pieces(owner, head):
        cut = head_cut(head)
        return [
            (source.at[owner], target.at[:, cut])
            for source, target in ((q_back, q_out), (k_back, k_out), (v_back, v_out))
        ]

    def back_copies(owner, head, out_index, in_index, device):
        return [
            remote(source, target, back_send.at[at, out_index], back_recv.at[at, in_index], device)
            for at, (source, target) in enumerate(back_pieces(owner, head))
        ]

    @pl.loop(0, count - 1)
    def _(turn):
        step = far_first(turn)
        peer = lax.rem(me + step, count)
        for copy in head_copies(row_pieces(peer, me), 0, step, me, (peer, core)):
            copy.start()

    owns = [
        pltpu.make_async_copy(source, target, local.at[4 + at])
        for at, (source, target) in enumerate(
            row_pieces(me, me) + plane_pieces(column, column)
        )
    ]
    for copy in owns:
        copy.start()
    for copy in loads:
        copy.wait()

    by_rows = (((1,), (1,)), ((), ()))
    by_columns = (((0,), (0,)), ((), ()))
    stat_rows = s_own.shape[2:]
    block_rows = rows // 2
    stat_at = lax.broadcasted_iota(jnp.int32, stat_rows, 0)
    early_half = lax.broadcasted_iota(jnp.int32, stat_rows, 1) < block_rows
    log_row = stat_at < 1

    @pl.loop(0, count)
    def _(turn):
        head = lax.rem(me + far_first(turn), count)
        grads = lax.dot_general(
            b_own[...], w_own[head_cut(head), :], by_rows, preferred_element_type=jnp.float32
        ).astype(low)
        g_own[head] = grads.reshape(2, block_rows, dim)
        product = grads.astype(jnp.float32) * a_own[:, head_cut(head)].astype(jnp.float32)
        deltas = lax.dot_general(
            jnp.ones((stat_rows[0], dim), jnp.float32), product, by_rows,
            precision=lax.Precision.HIGHEST, preferred_element_type=jnp.float32,
        )
        logs = jnp.broadcast_to(l_own[pl.ds(head, 1), :], stat_rows)
        stats = jnp.where(log_row, logs, deltas)
        turned = pltpu.roll(stats, block_rows, 1)
        s_own[head, 0] = jnp.where(early_half, stats, turned)
        s_own[head, 1] = jnp.where(early_half, turned, stats)

        @pl.when(turn > 0)
        def _():
            step = far_first(turn - 1)
            before = lax.rem(me + step, count)
            for copy in head_copies(grad_pieces(before, me), 3, step, me, (before, core)):
                copy.start()

    for group in range(groups):
        for step in range(1, side):
            to_column = plane_peer(step)
            device = (plane + to_column, core)
            for copy in group_of(
                plane_copies(to_column, column, step, column, device), group
            ):
                copy.start()

    g_all[owner_blocks(me)] = g_own[me]
    s_all[owner_blocks(me)] = s_own[me]

    for copy in owns:
        copy.wait()

    rows_all = side * rows

    def weight_part(part, grads_in):
        saved = a_all[:, :, pl.ds(part * dim, dim)].reshape(rows_all, dim)
        return lax.dot_general(
            saved, grads_in, by_columns, preferred_element_type=jnp.float32
        ).astype(low)

    def group_grads(to_core, group):
        cut = pl.ds(pl.multiple_of(to_core * half + group * sub, sub), sub)
        return b_all[:, :, cut].reshape(rows_all, sub)

    for group in range(groups):
        for step in range(1, side):
            to_column = plane_peer(step)
            device = (plane + to_column, core)
            for copy in group_of(
                plane_copies(column, to_column, step, to_column, device), group
            ):
                copy.wait_recv()
        for turn in range(1, cores):
            to_core = lax.rem(core + turn, cores)
            grads_in = group_grads(to_core, group)
            for part in range(side):
                w_core[group, to_core, part] = weight_part(part, grads_in)
            core_copy(group, to_core, core, turn).start()
        grads_in = group_grads(core, group)
        for part in range(side):
            w_land[group, core, part] = weight_part(part, grads_in)
        for turn in range(1, cores):
            other = lax.rem(core + turn, cores)
            core_copy(group, other, core, turn).wait_send()
            core_copy(group, core, other, turn).wait_recv()
        for part in range(side):
            merged = w_land[group, 0, part].astype(jnp.float32)
            for slot in range(1, cores):
                merged = merged + w_land[group, slot, part].astype(jnp.float32)
            w_part[group, part] = merged.astype(low)
        w_line[group, row] = w_part[group, row]
        for step in range(1, side):
            to_row = lax.rem(row + step, side)
            line_copy(
                group, to_row, row, step, row, (to_row * side + column, core)
            ).start()
    for step in range(1, side):
        to_column = plane_peer(step)
        device = (plane + to_column, core)
        for copy in plane_copies(to_column, column, step, column, device):
            copy.wait_send()

    @pl.loop(1, count)
    def _(step):
        peer = lax.rem(me + step, count)
        device = (peer, core)
        for copy in head_copies(row_pieces(peer, me), 0, step, me, device):
            copy.wait_send()
        for copy in head_copies(grad_pieces(peer, me), 3, step, me, device):
            copy.wait_send()
        for copy in head_copies(row_pieces(me, peer), 0, step, peer, device):
            copy.wait_recv()
        for copy in head_copies(grad_pieces(me, peer), 3, step, peer, device):
            copy.wait_recv()

    blocks = places.shape[0]
    length = count * rows
    for place in range(blocks):
        block = sources[place]
        target = pl.ds(place * block_rows, block_rows)
        for raw, ordered in ((q_all, q_row), (k_all, k_row), (v_all, v_row), (g_all, g_row)):
            ordered[target, :] = raw[block]
    for pair_at in range(blocks // 2):
        early = s_all[sources[2 * pair_at]]
        late = s_all[sources[2 * pair_at + 1]]
        s_row[pair_at] = jnp.where(early_half, early, late)
    tiles = length // tile
    per_tile = tile // rows
    tile_blocks = tile // block_rows
    dq[...] = jnp.zeros_like(dq)

    def pair(i, j, diagonal, sums):
        key_cut = pl.ds(j * tile, tile)
        query_cut = pl.ds(pl.multiple_of(i * tile, tile), tile)
        k_tile, v_tile = k_row[key_cut, :], v_row[key_cut, :]
        q_tile, g_tile = q_row[query_cut, :], g_row[query_cut, :]
        log_line = jnp.concatenate(
            [s_row[i * per_tile + m, 0:1, :] for m in range(per_tile)], axis=1
        )
        delta_line = jnp.concatenate(
            [s_row[i * per_tile + m, 1:2, :] for m in range(per_tile)], axis=1
        )
        scores = lax.dot_general(k_tile, q_tile, by_rows, preferred_element_type=jnp.float32)
        probs = jnp.exp(scores * scaling - log_line)
        if diagonal:
            key_at = lax.broadcasted_iota(jnp.int32, (tile, tile), 0)
            query_at = lax.broadcasted_iota(jnp.int32, (tile, tile), 1)
            probs = jnp.where(key_at <= query_at, probs, 0.0)
        dprobs = lax.dot_general(v_tile, g_tile, by_rows, preferred_element_type=jnp.float32)
        dscores = (probs * (dprobs - delta_line)).astype(low)
        dv_sum = sums[1] + jnp.dot(
            probs.astype(low), g_tile, preferred_element_type=jnp.float32
        )
        dk_sum = sums[0] + jnp.dot(dscores, q_tile, preferred_element_type=jnp.float32)
        dq[pl.ds(i * tile_blocks, tile_blocks)] += lax.dot_general(
            dscores, k_tile, by_columns, preferred_element_type=jnp.float32
        ).reshape(tile_blocks, block_rows, dim)
        return dk_sum, dv_sum

    for j in range(tiles):
        zero = jnp.zeros((tile, dim), jnp.float32)
        sums = pair(j, j, True, (zero, zero))
        if j + 1 < tiles:
            sums = lax.fori_loop(
                j + 1, tiles, lambda i, carry: pair(i, j, False, carry), sums
            )
        key_blocks = pl.ds(j * tile_blocks, tile_blocks)
        dk[key_blocks] = sums[0].reshape(tile_blocks, block_rows, dim)
        dv[key_blocks] = sums[1].reshape(tile_blocks, block_rows, dim)
    for block in range(blocks):
        place = places[block]
        target = pl.ds(block % 2 * block_rows, block_rows)
        q_back[block // 2, target, :] = (dq[place] * scaling).astype(low)
        k_back[block // 2, target, :] = (dk[place] * scaling).astype(low)
        v_back[block // 2, target, :] = dv[place].astype(low)

    @pl.loop(0, count - 1)
    def _(turn):
        step = far_first(turn)
        peer = lax.rem(me + step, count)
        for copy in back_copies(peer, me, step, me, (peer, core)):
            copy.start()

    returns = [
        pltpu.make_async_copy(source, target, local.at[at])
        for at, (source, target) in enumerate(back_pieces(me, me))
    ]
    for copy in returns:
        copy.start()

    for group in range(groups):
        for step in range(1, side):
            to_row = lax.rem(row + step, side)
            device = (to_row * side + column, core)
            line_copy(group, to_row, row, step, row, device).wait_send()
            line_copy(group, row, to_row, step, to_row, device).wait_recv()
        total = w_line[group, 0].astype(jnp.float32)
        for part in range(1, side):
            total = total + w_line[group, part].astype(jnp.float32)
        w_half[core, :, pl.ds(group * sub, sub)] = total.astype(low)

    def half_copy(slot, turn, other):
        return remote(
            w_half.at[slot], w_half.at[slot], half_send.at[turn], half_recv.at[slot], (me, other)
        )

    for turn in range(1, cores):
        half_copy(core, turn, lax.rem(core + turn, cores)).start()
    for turn in range(1, cores):
        other = lax.rem(core + turn, cores)
        half_copy(core, turn, other).wait_send()
        half_copy(other, turn, other).wait_recv()
    for slot in range(cores):
        w_out[:, pl.ds(slot * half, half)] = w_half[slot]

    for copy in returns:
        copy.wait()

    @pl.loop(1, count)
    def _(step):
        peer = lax.rem(me + step, count)
        for copy in back_copies(peer, me, step, me, (peer, core)):
            copy.wait_send()
        for copy in back_copies(me, peer, step, peer, (peer, core)):
            copy.wait_recv()


def head_per_device(
    side, cores, block_pos, queries, keys, values, attn_out, log_sums, grad_out, out_weight
):
    count = lax.axis_size("seq")
    rows = queries.shape[1]
    width = queries.shape[2]
    heads = log_sums.shape[1]
    dim = width // heads
    scaling = dim ** (-0.5)
    out_width = grad_out.shape[2]
    share = out_width // cores
    length = count * rows
    low = jnp.bfloat16
    table = block_pos[0]
    numbers = jnp.arange(table.shape[0], dtype=jnp.int32)
    inverse = jnp.sum(
        jnp.where(table[None, :] == numbers[:, None], numbers[None, :], 0), axis=1
    )
    block_rows = rows // 2
    groups = 2
    sub = share // groups
    pieces = side + groups * cores
    dma = pltpu.SemaphoreType.DMA
    tile = min(512, length)
    vmem = pl.BlockSpec(memory_space=pltpu.VMEM)
    wide = (length, dim)
    block_shape = (2 * count, block_rows, dim)
    split = (count, rows, dim)
    stat = (count, 8, rows)
    grad_queries, grad_keys, grad_values, weight_share = pl.pallas_call(
        functools.partial(fused_kernel, count, side, cores, dim, tile, scaling),
        out_shape=[jax.ShapeDtypeStruct((rows, width), low)] * 3
        + [jax.ShapeDtypeStruct((dim, out_width), low)],
        in_specs=[pl.BlockSpec(memory_space=pltpu.SMEM)] * 2 + [ANY] * 7,
        out_specs=[ANY] * 3 + [vmem],
        scratch_shapes=[pltpu.VMEM(block_shape, low)] * 4
        + [
            pltpu.VMEM((2 * count, 8, rows), jnp.float32),
            pltpu.VMEM((side, rows, side * dim), low),
            pltpu.VMEM((side, rows, out_width), low),
            pltpu.VMEM((rows, width), low),
            pltpu.VMEM((rows, out_width), low),
            pltpu.VMEM((heads, rows), jnp.float32),
            pltpu.VMEM(out_weight.shape, low),
            pltpu.VMEM((count, 2, block_rows, dim), low),
            pltpu.VMEM((count, 2, 8, rows), jnp.float32),
        ]
        + [pltpu.VMEM(wide, low)] * 4
        + [pltpu.VMEM(stat, jnp.float32)]
        + [pltpu.VMEM(block_shape, jnp.float32)] * 3
        + [pltpu.VMEM(split, low)] * 3
        + [pltpu.VMEM((groups, side, dim, sub), low)] * 2
        + [pltpu.VMEM((cores, dim, share), low)]
        + [pltpu.VMEM((groups, cores, side, dim, sub), low)] * 2
        + [
            dma((5, count)), dma((5, count)),
            dma((pieces, side)), dma((pieces, side)),
            dma((groups, side)), dma((groups, side)),
            dma((3, count)), dma((3, count)),
            dma((cores,)), dma((cores,)), dma((groups, cores)), dma((groups, cores)),
            dma((pieces + 7,)),
        ],
        compiler_params=pltpu.CompilerParams(
            collective_id=0, has_side_effects=True, vmem_limit_bytes=60 * 1024 * 1024
        ),
    )(
        inverse, table,
        *(part.reshape(2, block_rows, width) for part in (queries, keys, values)),
        attn_out[0], grad_out[0], log_sums[0],
        out_weight,
    )
    grad_queries, grad_keys, grad_values, weight_share = pl.pallas_call(
        leave_kernel,
        out_shape=[jax.ShapeDtypeStruct((rows, width), low)] * 3
        + [jax.ShapeDtypeStruct((dim, out_width), jnp.float32)],
        in_specs=[vmem] * 4,
        out_specs=[vmem] * 4,
    )(grad_queries, grad_keys, grad_values, weight_share)
    return grad_queries[None], grad_keys[None], grad_values[None], weight_share


def leave_kernel(q_in, k_in, v_in, w_in, q_out, k_out, v_out, w_out):
    for source, target in ((q_in, q_out), (k_in, k_out), (v_in, v_out), (w_in, w_out)):
        target[...] = source[...].astype(target.dtype)


def make_per_device(mesh):
    count = mesh.shape["seq"]
    cores = mesh.shape["dp"]
    side = int(round(count ** 0.5))

    def per_device(block_pos, queries, keys, values, attn_out, log_sums, grad_out, out_weight):
        heads = log_sums.shape[1]
        arguments = (
            block_pos, queries, keys, values, attn_out, log_sums, grad_out, out_weight
        )
        if heads == count and side * side == count:
            return head_per_device(side, cores, *arguments)
        return grid_per_device(*arguments)

    return per_device


def solution(mesh):
    in_specs = (
        P("dp", None),
        P("dp", "seq", None),
        P("dp", "seq", None),
        P("dp", "seq", None),
        P("dp", "seq", None),
        P("dp", None, "seq"),
        P("dp", "seq", None),
        P(),
    )
    out_specs = (P("dp", "seq", None), P("dp", "seq", None), P("dp", "seq", None), P("seq", None))
    return jax.shard_map(
        make_per_device(mesh), mesh=mesh, in_specs=in_specs, out_specs=out_specs, check_vma=False
    )
```

profile of v0, /device:TPU:16, one launch (start us, length us, event | category | flops | bytes accessed | tf_op | source)
XLA Modules:
  0.0 123.5 jit_solution(15054501443321794390)
XLA Ops:
  0.6 1.3 %select_reduce_fusion.sources = s32[32]{0:T(128)} fusion(s32[32]{0:T(128)} %bitcast.16), kind=kLoop, calls=%fused_computation | loop fusion | flops 3040 | bytes 256 | tf_op jit(solution)/shard_map/reduce_sum | solution.py:556
  1.9 118.5 %shard_map.111 = (bf16[128,2048]{1,0:T(8,128)(2,1)}, bf16[128,2048]{1,0:T(8,128)(2,1)}, bf16[128,2048]{1,0:T(8,128)(2,1)}, bf16[128,2048]{1,0:T(8,128)(2,1)}) custom-call(s32[32]{0:T(128)} %select_reduce_fusion.sources, s32[32]{0:T(128)} %bitcast.17, bf16[2,64,2048]{2,1,0:T(8,128)(2,1)} %bitcast.10, bf16[2,64,2048]{2,1,0:T(8,128)(2,1)} %bitcast.11, ...), custom_call_target="tpu_custom_call" | custom-call | tf_op jit(solution)/shard_map/pallas_call | solution.py:570
  120.4 3.0 %shard_map.112 = (bf16[128,2048]{1,0:T(8,128)(2,1)}, bf16[128,2048]{1,0:T(8,128)(2,1)}, bf16[128,2048]{1,0:T(8,128)(2,1)}, f32[128,2048]{1,0:T(8,128)}) custom-call(bf16[128,2048]{1,0:T(8,128)(2,1)} %get-tuple-element.12.q_in, bf16[128,2048]{1,0:T(8,128)(2,1)} %get-tuple-element.13.k_in, bf16[128,2048]{1,0:T(8,128)(2,1)} %get-tuple-element.14.v_in, ...), custom_call_target="tpu_custom_call" | custom-call | tf_op jit(solution)/shard_map/pallas_call | solution.py:612
where the time goes:
time: 124 us; the launch traced here: 123 us
  Pallas kernels  122 us (98%)
  other arithmetic  1.28 us (1%)
    pallas_call x1, Pallas kernels, head_per_device(): pl.pallas_call(functools.partial(fused_kernel, count, side, cores, dim, t...  119 us
    pallas_call x1, Pallas kernels, head_per_device(): pl.pallas_call(leave_kernel, out_shape=[jax.ShapeDtypeStruct((rows, width...  3.04 us

commit v1 on v0

v1 whole, which is shorter than its diff:
```python
import functools

import jax
import jax.numpy as jnp
from jax import lax
from jax.experimental import pallas as pl
from jax.experimental.pallas import tpu as pltpu
from jax.sharding import PartitionSpec as P


def shifted(shard, axis, by):
    count = lax.axis_size(axis)
    return lax.ppermute(shard, axis, [(i, (i + by) % count) for i in range(count)])


def slot_positions(table_row, owners, half_rows):
    slot_ids = owners[:, None] * 2 + jnp.arange(2, dtype=jnp.int32)[None, :]
    pick_rows = (
        slot_ids[:, :, None] == jnp.arange(table_row.shape[0], dtype=jnp.int32)[None, None, :]
    ).astype(jnp.int32)
    block_ids = jnp.sum(pick_rows * table_row[None, None, :], axis=-1)
    offsets = jnp.arange(half_rows, dtype=jnp.int32)
    return (block_ids[:, :, None] * half_rows + offsets[None, None, :]).reshape(
        owners.shape[0], 2 * half_rows
    )


def block_core(
    query_rows, grad_rows, log_block, delta_block, key_rows, value_rows, allowed, scaling
):
    head_count = log_block.shape[0]
    query_len = query_rows.shape[0]
    key_len = key_rows.shape[0]
    query_heads = query_rows.reshape(query_len, head_count, -1)
    grad_split = grad_rows.reshape(query_len, head_count, -1)
    key_heads = key_rows.reshape(key_len, head_count, -1)
    value_heads = value_rows.reshape(key_len, head_count, -1)
    scores = (
        jnp.einsum("ahd,bhd->hab", query_heads, key_heads, preferred_element_type=jnp.float32)
        * scaling
    )
    attn_probs = jnp.where(allowed[None], jnp.exp(scores - log_block[:, :, None]), 0.0)
    probs_low = attn_probs.astype(jnp.bfloat16)
    dprobs = jnp.einsum("ahd,bhd->hab", grad_split, value_heads, preferred_element_type=jnp.float32)
    dscores = attn_probs * (dprobs - delta_block[:, :, None])
    dscores_low = dscores.astype(jnp.bfloat16)
    value_part = jnp.einsum(
        "hab,ahd->bhd", probs_low, grad_split, preferred_element_type=jnp.float32
    )
    key_part = (
        jnp.einsum("hab,ahd->bhd", dscores_low, query_heads, preferred_element_type=jnp.float32)
        * scaling
    )
    query_part = (
        jnp.einsum("hab,bhd->ahd", dscores_low, key_heads, preferred_element_type=jnp.float32)
        * scaling
    )
    return (
        query_part.reshape(query_len, -1),
        key_part.reshape(key_len, -1),
        value_part.reshape(key_len, -1),
    )


def block_grads(
    query_rows, grad_rows, log_block, delta_block, key_rows, value_rows, allowed, scaling
):
    parts = block_core(
        query_rows, grad_rows, log_block, delta_block, key_rows, value_rows, allowed, scaling
    )
    return (parts[0], parts[1].astype(jnp.bfloat16), parts[2].astype(jnp.bfloat16))


def grid_per_device(block_pos, queries, keys, values, attn_out, log_sums, grad_out, out_weight):
    dev_count = lax.axis_size("seq")
    grid_side = 4 + 4 * (dev_count // 64)
    my_index = lax.axis_index("seq")
    table_row = block_pos[0]
    own_queries = queries[0]
    tok_rows = own_queries.shape[0]
    half_rows = tok_rows // 2
    head_count = log_sums.shape[1]
    width_all = own_queries.shape[1]
    scaling = (width_all // head_count) ** (-0.5)
    cotangent = grad_out[0]
    grad_heads = lax.dot_general(
        cotangent, out_weight, (((1,), (1,)), ((), ())), preferred_element_type=jnp.float32
    ).astype(jnp.bfloat16)
    deltas = jnp.einsum(
        "ahd,ahd->ha",
        grad_heads.reshape(tok_rows, head_count, -1),
        attn_out[0].reshape(tok_rows, head_count, -1),
        preferred_element_type=jnp.float32,
    )
    query_pack = (own_queries[None], grad_heads[None], log_sums[0][None], deltas[None])
    key_pack = (keys[0][None], values[0][None])
    query_list = [query_pack]
    key_list = [key_pack]
    for offset in range(1, grid_side):
        query_list.append(
            (
                shifted(query_pack[0].astype(jnp.float32), "seq", offset).astype(jnp.bfloat16),
                shifted(query_pack[1].astype(jnp.float32), "seq", offset).astype(jnp.bfloat16),
                shifted(query_pack[2], "seq", offset),
                shifted(query_pack[3], "seq", offset),
            )
        )
        key_list.append(shifted((key_pack[0], key_pack[1]), "seq", offset * grid_side))
    query_stack = tuple(
        (jnp.concatenate([parcel[member] for parcel in query_list], axis=0) for member in range(4))
    )
    key_stack = tuple(
        (jnp.concatenate([parcel[member] for parcel in key_list], axis=0) for member in range(2))
    )
    query_rows = query_stack[0].reshape(-1, width_all)
    grad_rows = query_stack[1].reshape(-1, width_all)
    log_block = jnp.transpose(query_stack[2], (1, 0, 2)).reshape(head_count, -1)
    delta_block = jnp.transpose(query_stack[3], (1, 0, 2)).reshape(head_count, -1)
    query_owners = (my_index - jnp.arange(grid_side, dtype=jnp.int32)) % dev_count
    key_owners = (my_index - jnp.arange(grid_side, dtype=jnp.int32) * grid_side) % dev_count
    query_pos = slot_positions(table_row, query_owners, half_rows).reshape(-1)
    key_pos = slot_positions(table_row, key_owners, half_rows)
    query_total = jnp.zeros((grid_side * tok_rows, width_all), jnp.float32)
    key_results = []
    for offset in range(grid_side):
        key_now = key_stack[0][offset]
        value_now = key_stack[1][offset]
        allowed = key_pos[offset][None, :] <= query_pos[:, None]
        results = block_grads(
            query_rows, grad_rows, log_block, delta_block, key_now, value_now, allowed, scaling
        )
        query_total = query_total + results[0]
        key_results.append((results[1], results[2]))
    query_parts = query_total.astype(jnp.bfloat16).reshape(grid_side, tok_rows, width_all)
    query_sum = query_parts[0].astype(jnp.float32)
    for offset in range(1, grid_side):
        query_sum = query_sum + shifted(query_parts[offset], "seq", -offset).astype(jnp.float32)
    key_sum = key_results[0][0].astype(jnp.float32)
    value_sum = key_results[0][1].astype(jnp.float32)
    for offset in range(1, grid_side):
        returned = shifted(
            (key_results[offset][0], key_results[offset][1]), "seq", -offset * grid_side
        )
        key_sum = key_sum + returned[0].astype(jnp.float32)
        value_sum = value_sum + returned[1].astype(jnp.float32)
    columns = attn_out[0]
    weight_share = lax.psum_scatter(
        lax.dot_general(
            columns, cotangent, (((0,), (0,)), ((), ())), preferred_element_type=jnp.float32
        ),
        ("seq", "dp"),
        scatter_dimension=0,
        tiled=True,
    )
    weight_share = lax.all_gather(
        weight_share.astype(jnp.bfloat16), "dp", axis=0, tiled=True
    ).astype(weight_share.dtype)
    return (
        query_sum.astype(jnp.bfloat16)[None],
        key_sum.astype(jnp.bfloat16)[None],
        value_sum.astype(jnp.bfloat16)[None],
        weight_share,
    )


MESH = pl.DeviceIdType.MESH
ANY = pl.BlockSpec(memory_space=pl.ANY)


def enter(count, side, cores, me, core, plane):
    barrier = pltpu.get_barrier_semaphore()
    peers = [(lax.rem(me + step, count), core) for step in range(1, count)]
    for turn in range(1, cores):
        peers += [(plane + column, lax.rem(core + turn, cores)) for column in range(side)]
    for peer in peers:
        pl.semaphore_signal(barrier, inc=1, device_id=peer, device_id_type=MESH)
    pl.semaphore_wait(barrier, len(peers))


def fused_kernel(
    count, side, cores, dim, tile, scaling,
    places, q_in, k_in, v_in, a_in, b_in, l_in, w_in,
    q_out, k_out, v_out, w_out,
    q_all, k_all, v_all, g_all, l_all, d_all, a_all, b_all, a_turned,
    a_own, b_own, l_own, w_own, g_own, log_own, delta_own,
    q_row, k_row, v_row, g_row, l_row, d_row, probs_all, dq, dk, dv,
    q_back, k_back, v_back, w_part, w_near, w_mid, w_far, w_half, sources,
    send, recv, a_send, a_recv, b_send, b_recv, pass_send, pass_recv,
    near_send, near_recv, far_send, far_recv,
    back_send, back_recv, half_send, half_recv, local,
):
    me = lax.axis_index("seq")
    core = lax.axis_index("dp")
    column = lax.rem(me, side)
    plane = me - column
    row = me // side
    groups, _, _, sub = w_part.shape
    low = jnp.bfloat16
    near_side = side // 2
    near_base = (row // near_side) * near_side
    near_at = row - near_base
    mirror = side - 1 - row

    loads = [
        pltpu.make_async_copy(source, target, local.at[at])
        for at, (source, target) in enumerate(
            [(l_in, l_own), (b_in, b_own), (w_in, w_own), (a_in, a_own)]
        )
    ]
    for copy in loads:
        copy.start()
    enter(count, side, cores, me, core, plane)

    def head_cut(head):
        return pl.ds(pl.multiple_of(head * dim, dim), dim)

    rows = a_own.shape[0]
    block_rows = rows // 2
    blocks = 2 * count

    def owner_blocks(owner):
        return pl.ds(owner * 2, 2)

    def remote(source, target, sender, receiver, device):
        return pltpu.make_async_remote_copy(
            source, target, sender, receiver, device_id=device, device_id_type=MESH
        )

    def piece(kind, head, owner):
        cut = head_cut(head)
        at = owner_blocks(owner)
        if kind == 0:
            return q_in.at[:, :, cut], q_all.at[at]
        if kind == 1:
            return k_in.at[:, :, cut], k_all.at[at]
        if kind == 2:
            return v_in.at[:, :, cut], v_all.at[at]
        if kind == 3:
            return log_own.at[head], l_all.at[at]
        if kind == 4:
            return g_own.at[head], g_all.at[at]
        return delta_own.at[head], d_all.at[at]

    def outgoing(kind, step):
        peer = lax.rem(me + step, count)
        source, target = piece(kind, peer, me)
        return remote(source, target, send.at[kind, step], recv.at[kind, me], (peer, core))

    def incoming(kind, step):
        peer = lax.rem(me + step, count)
        source, target = piece(kind, me, peer)
        return remote(source, target, send.at[kind, step], recv.at[kind, peer], (peer, core))

    def await_pieces(kinds):
        @pl.loop(1, count)
        def _(step):
            for kind in kinds:
                incoming(kind, step).wait_recv()

    def a_piece(part, to_column, slot):
        return (
            a_in.at[:, head_cut(part * side + to_column)],
            a_all.at[core, slot, :, pl.ds(part * dim, dim)],
        )

    def b_piece(group, to_core, sequence, slot):
        at = pl.ds(pl.multiple_of((to_core * groups + group) * sub, sub), sub)
        return b_in.at[:, at], b_all.at[sequence, slot, :, pl.ds(group * sub, sub)]

    def a_outgoing(part, step):
        to_column = plane_peer(step)
        source, target = a_piece(part, to_column, column)
        return remote(
            source, target, a_send.at[part, step], a_recv.at[part, column],
            (plane + to_column, core),
        )

    def a_incoming(part, step):
        slot = plane_peer(step)
        source, target = a_piece(part, column, slot)
        return remote(
            source, target, a_send.at[part, step], a_recv.at[part, slot], (plane + slot, core)
        )

    def a_pass(sequence, slot, turn):
        block = a_all.at[sequence, slot]
        return remote(
            block, block, pass_send.at[slot, turn], pass_recv.at[slot, sequence],
            (me, lax.rem(core + turn, cores)),
        )

    def b_outgoing(group, step, turn):
        to_column = plane_peer(step)
        to_core = lax.rem(core + turn, cores)
        source, target = b_piece(group, to_core, core, column)
        return remote(
            source, target, b_send.at[group, step, turn], b_recv.at[group, column, core],
            (plane + to_column, to_core),
        )

    def b_incoming(group, step, turn):
        slot = plane_peer(step)
        sequence = lax.rem(core + turn, cores)
        source, target = b_piece(group, core, sequence, slot)
        return remote(
            source, target, b_send.at[group, step, turn], b_recv.at[group, slot, sequence],
            (plane + slot, sequence),
        )

    b_routes = [
        (step, turn) for step in range(side) for turn in range(cores) if step + turn > 0
    ]

    def plane_peer(step):
        return lax.rem(column + step, side)

    def far_first(turn):
        far = count - side
        return jnp.where(turn < far, turn + side, lax.rem(turn - far + 1, side))

    def near_peer(step):
        return near_base + lax.rem(near_at + step, near_side)

    def near_copies(group, to_row, slot, out_index, in_index, device):
        return [
            remote(
                w_part.at[group, part], w_near.at[group, slot, at],
                near_send.at[group, out_index, at], near_recv.at[group, in_index, at], device,
            )
            for at, part in enumerate((to_row, side - 1 - to_row))
        ]

    def far_copy(group):
        return remote(
            w_mid.at[group], w_far.at[group], far_send.at[group], far_recv.at[group],
            (mirror * side + column, core),
        )

    backs = ((q_back, q_out), (k_back, k_out), (v_back, v_out))

    def back_copy(at, owner, head, out_index, in_index, device):
        source, target = backs[at]
        return remote(
            source.at[owner], target.at[:, head_cut(head)],
            back_send.at[at, out_index], back_recv.at[at, in_index], device,
        )

    def start_returns(kinds):
        @pl.loop(0, count - 1)
        def _(turn):
            step = far_first(turn)
            peer = lax.rem(me + step, count)
            for at in kinds:
                back_copy(at, peer, me, step, me, (peer, core)).start()

        for at in kinds:
            source, target = backs[at]
            pltpu.make_async_copy(
                source.at[me], target.at[:, head_cut(me)], local.at[at]
            ).start()

    @pl.loop(0, count - 1)
    def _(turn):
        step = far_first(turn)
        for kind in (0, 1):
            outgoing(kind, step).start()

    for step in range(1, side):
        for part in range(side):
            a_outgoing(part, step).start()
    owns = [
        pltpu.make_async_copy(source, target, local.at[4 + at])
        for at, (source, target) in enumerate(
            [a_piece(part, column, column) for part in range(side)]
            + [b_piece(group, core, core, column) for group in range(groups)]
            + [piece(kind, me, me) for kind in range(3)]
        )
    ]
    for copy in owns:
        copy.start()
    loads[0].wait()
    early_half = lax.broadcasted_iota(jnp.int32, (1, rows), 1) < block_rows
    for head in range(count):
        logs = l_own[head : head + 1, :]
        turned = pltpu.roll(logs, block_rows, 1)
        log_own[head, 0] = jnp.where(early_half, logs, turned)
        log_own[head, 1] = jnp.where(early_half, turned, logs)

    @pl.loop(0, count - 1)
    def _(turn):
        outgoing(3, far_first(turn)).start()

    l_all[owner_blocks(me)] = log_own[me]
    for copy in loads[1:]:
        copy.wait()

    by_rows = (((1,), (1,)), ((), ()))
    by_columns = (((0,), (0,)), ((), ()))

    @pl.loop(0, count)
    def _(turn):
        head = lax.rem(me + far_first(turn), count)
        grads = lax.dot_general(
            b_own[...], w_own[head_cut(head), :], by_rows, preferred_element_type=jnp.float32
        ).astype(low)
        g_own[head] = grads.reshape(2, block_rows, dim)
        product = grads.astype(jnp.float32) * a_own[:, head_cut(head)].astype(jnp.float32)
        deltas = lax.dot_general(
            jnp.ones((8, dim), jnp.float32), product, by_rows,
            precision=lax.Precision.HIGHEST, preferred_element_type=jnp.float32,
        )[0:1]
        turned = pltpu.roll(deltas, block_rows, 1)
        delta_own[head, 0] = jnp.where(early_half, deltas, turned)
        delta_own[head, 1] = jnp.where(early_half, turned, deltas)

        @pl.when(turn > 0)
        def _():
            step = far_first(turn - 1)
            for kind in (4, 5):
                outgoing(kind, step).start()

    g_all[owner_blocks(me)] = g_own[me]
    d_all[owner_blocks(me)] = delta_own[me]

    @pl.loop(0, count - 1)
    def _(turn):
        outgoing(2, far_first(turn)).start()

    for group in range(groups):
        for step, turn in b_routes:
            b_outgoing(group, step, turn).start()

    @pl.loop(0, blocks)
    def _(place):
        found = 0
        for block in range(blocks):
            found = jnp.where(places[0, block] == place, block, found)
        sources[place] = found

    for copy in owns:
        copy.wait()
    def in_order(pairs):
        for place in range(blocks):
            block = sources[place]
            for raw, ordered in pairs:
                ordered[pl.ds(place * block_rows, block_rows), :] = raw[block]

    def in_order_lines(raw, ordered):
        for pair_at in range(blocks // 2):
            early = raw[sources[2 * pair_at]]
            late = raw[sources[2 * pair_at + 1]]
            ordered[pair_at] = jnp.where(early_half, early, late)

    length = count * rows
    tiles = length // tile
    per_tile = tile // rows
    tile_blocks = tile // block_rows
    pairs = tiles * (tiles + 1) // 2

    def pair_of(at):
        j = 0
        for later in range(1, tiles):
            j = j + jnp.where(at >= later * tiles - later * (later - 1) // 2, 1, 0)
        return at - (j * tiles - j * (j - 1) // 2) + j, j

    def cut(at):
        return pl.ds(pl.multiple_of(at * tile, tile), tile)

    def line(ordered, i):
        return jnp.concatenate([ordered[i * per_tile + m] for m in range(per_tile)], axis=1)

    await_pieces((0, 1, 3))
    in_order(((q_all, q_row), (k_all, k_row)))
    in_order_lines(l_all, l_row)

    @pl.loop(0, pairs)
    def _(at):
        i, j = pair_of(at)
        scores = lax.dot_general(
            k_row[cut(j), :], q_row[cut(i), :], by_rows, preferred_element_type=jnp.float32
        )
        key_at = lax.broadcasted_iota(jnp.int32, (tile, tile), 0)
        query_at = lax.broadcasted_iota(jnp.int32, (tile, tile), 1)
        allowed = key_at - query_at <= (i - j) * tile
        probs_all[at] = jnp.where(allowed, jnp.exp(scores * scaling - line(l_row, i)), 0.0)

    rows_all = cores * side * rows

    def weight_stage(group):
        for step, turn in b_routes:
            b_incoming(group, step, turn).wait_recv()
        grads_in = b_all[:, :, :, pl.ds(group * sub, sub)].reshape(rows_all, sub)
        w_part[group] = (
            jnp.dot(a_turned[...], grads_in, preferred_element_type=jnp.float32)
            .astype(low)
            .reshape(side, dim, sub)
        )
        for step in range(1, near_side):
            to_row = near_peer(step)
            device = (to_row * side + column, core)
            for copy in near_copies(group, to_row, near_at, step, near_at, device):
                copy.start()

    def near_sum(group, part, at):
        total = w_part[group, part].astype(jnp.float32)
        for step in range(1, near_side):
            slot = lax.rem(near_at + step, near_side)
            total = total + w_near[group, slot, at].astype(jnp.float32)
        return total

    def cross_stage(group):
        for step in range(1, near_side):
            to_row = near_peer(step)
            device = (to_row * side + column, core)
            for copy in near_copies(group, to_row, near_at, step, near_at, device):
                copy.wait_send()
            slot = to_row - near_base
            for copy in near_copies(group, row, slot, step, slot, device):
                copy.wait_recv()
        w_mid[group] = near_sum(group, mirror, 1).astype(low)
        far_copy(group).start()

    for step in range(side):
        slot = plane_peer(step)
        if step > 0:
            for part in range(side):
                a_incoming(part, step).wait_recv()
        for turn in range(1, cores):
            a_pass(core, slot, turn).start()

    await_pieces((4, 5))
    in_order(((g_all, g_row),))
    in_order_lines(d_all, d_row)
    dv[...] = jnp.zeros_like(dv)
    dk[...] = jnp.zeros_like(dk)
    dq[...] = jnp.zeros_like(dq)

    def add_blocks(total, at, value):
        total[pl.ds(at * tile_blocks, tile_blocks)] += value.reshape(tile_blocks, block_rows, dim)

    @pl.loop(0, pairs)
    def _(at):
        i, j = pair_of(at)
        add_blocks(
            dv, j,
            jnp.dot(probs_all[at].astype(low), g_row[cut(i), :], preferred_element_type=jnp.float32),
        )

    for block in range(blocks):
        target = pl.ds(block % 2 * block_rows, block_rows)
        v_back[block // 2, target, :] = dv[places[0, block]].astype(low)
    start_returns((2,))

    for turn in range(1, cores):
        for slot in range(side):
            a_pass(lax.rem(core + turn, cores), slot, turn).wait_recv()
    for sequence in range(cores):
        for slot in range(side):
            at = pl.ds((sequence * side + slot) * rows, rows)
            a_turned[:, at] = a_all[sequence, slot].T

    await_pieces((2,))
    in_order(((v_all, v_row),))

    @pl.loop(0, pairs)
    def _(at):
        i, j = pair_of(at)
        q_tile, k_tile = q_row[cut(i), :], k_row[cut(j), :]
        dprobs = lax.dot_general(
            v_row[cut(j), :], g_row[cut(i), :], by_rows, preferred_element_type=jnp.float32
        )
        dscores = (probs_all[at] * (dprobs - line(d_row, i))).astype(low)
        add_blocks(dk, j, jnp.dot(dscores, q_tile, preferred_element_type=jnp.float32))
        add_blocks(
            dq, i,
            lax.dot_general(dscores, k_tile, by_columns, preferred_element_type=jnp.float32),
        )

    for block in range(blocks):
        target = pl.ds(block % 2 * block_rows, block_rows)
        k_back[block // 2, target, :] = (dk[places[0, block]] * scaling).astype(low)
    start_returns((1,))
    for block in range(blocks):
        target = pl.ds(block % 2 * block_rows, block_rows)
        q_back[block // 2, target, :] = (dq[places[0, block]] * scaling).astype(low)
    weight_stage(0)
    weight_stage(1)
    start_returns((0,))
    cross_stage(0)
    cross_stage(1)

    for step in range(1, side):
        for part in range(side):
            a_outgoing(part, step).wait_send()
    for turn in range(1, cores):
        for slot in range(side):
            a_pass(core, slot, turn).wait_send()
    for group in range(groups):
        for step, turn in b_routes:
            b_outgoing(group, step, turn).wait_send()

    @pl.loop(1, count)
    def _(step):
        for kind in range(6):
            outgoing(kind, step).wait_send()

    def half_copy(group, slot, turn, other):
        block = w_half.at[group, slot]
        return remote(
            block, block, half_send.at[group, turn], half_recv.at[group, slot], (me, other)
        )

    for group in range(groups):
        far_copy(group).wait_send()
        far_copy(group).wait_recv()
        total = near_sum(group, row, 0) + w_far[group].astype(jnp.float32)
        w_half[group, core] = total.astype(low)
        for turn in range(1, cores):
            half_copy(group, core, turn, lax.rem(core + turn, cores)).start()
    for group in range(groups):
        for turn in range(1, cores):
            other = lax.rem(core + turn, cores)
            half_copy(group, core, turn, other).wait_send()
            half_copy(group, other, turn, other).wait_recv()
        for slot in range(cores):
            w_out[:, pl.ds((slot * groups + group) * sub, sub)] = w_half[group, slot]

    for at, (source, target) in enumerate(backs):
        pltpu.make_async_copy(source.at[me], target.at[:, head_cut(me)], local.at[at]).wait()

    @pl.loop(1, count)
    def _(step):
        peer = lax.rem(me + step, count)
        for at in range(3):
            back_copy(at, peer, me, step, me, (peer, core)).wait_send()
            back_copy(at, me, peer, step, peer, (peer, core)).wait_recv()


def head_per_device(
    side, cores, block_pos, queries, keys, values, attn_out, log_sums, grad_out, out_weight
):
    count = lax.axis_size("seq")
    rows = queries.shape[1]
    width = queries.shape[2]
    heads = log_sums.shape[1]
    dim = width // heads
    scaling = dim ** (-0.5)
    out_width = grad_out.shape[2]
    share = out_width // cores
    length = count * rows
    low = jnp.bfloat16
    block_rows = rows // 2
    groups = 2
    sub = share // groups
    near_side = side // 2
    dma = pltpu.SemaphoreType.DMA
    tile = min(512, length)
    tiles = length // tile
    vmem = pl.BlockSpec(memory_space=pltpu.VMEM)
    wide = (length, dim)
    block_shape = (2 * count, block_rows, dim)
    split = (count, rows, dim)
    lines = (2 * count, 1, rows)
    own_lines = (count, 2, 1, rows)
    grad_queries, grad_keys, grad_values, weight_share = pl.pallas_call(
        functools.partial(fused_kernel, count, side, cores, dim, tile, scaling),
        out_shape=[jax.ShapeDtypeStruct((rows, width), low)] * 3
        + [jax.ShapeDtypeStruct((dim, out_width), low)],
        in_specs=[pl.BlockSpec(memory_space=pltpu.SMEM)] + [ANY] * 7,
        out_specs=[ANY] * 3 + [vmem],
        scratch_shapes=[pltpu.VMEM(block_shape, low)] * 4
        + [pltpu.VMEM(lines, jnp.float32)] * 2
        + [
            pltpu.VMEM((cores, side, rows, side * dim), low),
            pltpu.VMEM((cores, side, rows, share), low),
            pltpu.VMEM((side * dim, cores * side * rows), low),
            pltpu.VMEM((rows, width), low),
            pltpu.VMEM((rows, out_width), low),
            pltpu.VMEM((heads, rows), jnp.float32),
            pltpu.VMEM(out_weight.shape, low),
            pltpu.VMEM((count, 2, block_rows, dim), low),
        ]
        + [pltpu.VMEM(own_lines, jnp.float32)] * 2
        + [pltpu.VMEM(wide, low)] * 4
        + [pltpu.VMEM((count, 1, rows), jnp.float32)] * 2
        + [pltpu.VMEM((tiles * (tiles + 1) // 2, tile, tile), jnp.float32)]
        + [pltpu.VMEM(block_shape, jnp.float32)] * 3
        + [pltpu.VMEM(split, low)] * 3
        + [pltpu.VMEM((groups, side, dim, sub), low)]
        + [pltpu.VMEM((groups, near_side, 2, dim, sub), low)]
        + [pltpu.VMEM((groups, dim, sub), low)] * 2
        + [pltpu.VMEM((groups, cores, dim, sub), low)]
        + [pltpu.SMEM((2 * count,), jnp.int32)]
        + [
            dma((6, count)), dma((6, count)),
            dma((side, side)), dma((side, side)),
            dma((groups, side, cores)), dma((groups, side, cores)),
            dma((side, cores)), dma((side, cores)),
            dma((groups, near_side, 2)), dma((groups, near_side, 2)),
            dma((groups,)), dma((groups,)),
            dma((3, count)), dma((3, count)),
            dma((groups, cores)), dma((groups, cores)), dma((side + groups + 7,)),
        ],
        compiler_params=pltpu.CompilerParams(
            collective_id=0, has_side_effects=True, vmem_limit_bytes=60 * 1024 * 1024
        ),
    )(
        block_pos,
        *(part.reshape(2, block_rows, width) for part in (queries, keys, values)),
        attn_out[0], grad_out[0], log_sums[0],
        out_weight,
    )
    grad_queries, grad_keys, grad_values, weight_share = pl.pallas_call(
        leave_kernel,
        out_shape=[jax.ShapeDtypeStruct((rows, width), low)] * 3
        + [jax.ShapeDtypeStruct((dim, out_width), jnp.float32)],
        in_specs=[vmem] * 4,
        out_specs=[vmem] * 4,
    )(grad_queries, grad_keys, grad_values, weight_share)
    return grad_queries[None], grad_keys[None], grad_values[None], weight_share


def leave_kernel(q_in, k_in, v_in, w_in, q_out, k_out, v_out, w_out):
    for source, target in ((q_in, q_out), (k_in, k_out), (v_in, v_out), (w_in, w_out)):
        target[...] = source[...].astype(target.dtype)


def make_per_device(mesh):
    count = mesh.shape["seq"]
    cores = mesh.shape["dp"]
    side = int(round(count ** 0.5))

    def per_device(block_pos, queries, keys, values, attn_out, log_sums, grad_out, out_weight):
        heads = log_sums.shape[1]
        arguments = (
            block_pos, queries, keys, values, attn_out, log_sums, grad_out, out_weight
        )
        if heads == count and side * side == count and side % 2 == 0:
            return head_per_device(side, cores, *arguments)
        return grid_per_device(*arguments)

    return per_device


def solution(mesh):
    in_specs = (
        P("dp", None),
        P("dp", "seq", None),
        P("dp", "seq", None),
        P("dp", "seq", None),
        P("dp", "seq", None),
        P("dp", None, "seq"),
        P("dp", "seq", None),
        P(),
    )
    out_specs = (P("dp", "seq", None), P("dp", "seq", None), P("dp", "seq", None), P("seq", None))
    return jax.shard_map(
        make_per_device(mesh), mesh=mesh, in_specs=in_specs, out_specs=out_specs, check_vma=False
    )
```

time: 124 us -> 110 us (0.89)
  the two profiles are of different devices: /device:TPU:16 before, /device:TPU:0 now
where the time goes in v1:
time: 110 us
  Pallas kernels  110 us (100%)
    pallas_call x1, Pallas kernels, head_per_device(): pl.pallas_call(functools.partial(fused_kernel, count, side, cores, dim, t...  107 us
    pallas_call x1, Pallas kernels, head_per_device(): pl.pallas_call(leave_kernel, out_shape=[jax.ShapeDtypeStruct((rows, width...  3.04 us

profile of v1, /device:TPU:0, one launch (start us, length us, event | category | flops | bytes accessed | tf_op | source)
XLA Modules:
  0.0 110.3 jit_solution(5619622020016808095)
XLA Ops:
  0.6 106.6 %shard_map.111 = (bf16[128,2048]{1,0:T(8,128)(2,1)}, bf16[128,2048]{1,0:T(8,128)(2,1)}, bf16[128,2048]{1,0:T(8,128)(2,1)}, bf16[128,2048]{1,0:T(8,128)(2,1)}) custom-call(s32[1,32]{1,0:T(1,128)} %places.1, bf16[2,64,2048]{2,1,0:T(8,128)(2,1)} %bitcast.9, bf16[2,64,2048]{2,1,0:T(8,128)(2,1)} %bitcast.10, bf16[2,64,2048]{2,1,0:T(8,128)(2,1)} %bitcast.11, ...), custom_call_target="tpu_custom_call" | custom-call | tf_op jit(solution)/shard_map/pallas_call | solution.py:665
  107.3 3.0 %shard_map.112 = (bf16[128,2048]{1,0:T(8,128)(2,1)}, bf16[128,2048]{1,0:T(8,128)(2,1)}, bf16[128,2048]{1,0:T(8,128)(2,1)}, f32[128,2048]{1,0:T(8,128)}) custom-call(bf16[128,2048]{1,0:T(8,128)(2,1)} %get-tuple-element.12.q_in, bf16[128,2048]{1,0:T(8,128)(2,1)} %get-tuple-element.13.k_in, bf16[128,2048]{1,0:T(8,128)(2,1)} %get-tuple-element.14.v_in, ...), custom_call_target="tpu_custom_call" | custom-call | tf_op jit(solution)/shard_map/pallas_call | solution.py:713

commit v2 on v1

--- a/solution.py
+++ b/solution.py
@@ -183,8 +183,8 @@
     q_out, k_out, v_out, w_out,
     q_all, k_all, v_all, g_all, l_all, d_all, a_all, b_all, a_turned,
     a_own, b_own, l_own, w_own, g_own, log_own, delta_own,
-    q_row, k_row, v_row, g_row, l_row, d_row, probs_all, dq, dk, dv,
-    q_back, k_back, v_back, w_part, w_near, w_mid, w_far, w_half, sources,
+    q_row, k_row, v_row, g_row, l_row, d_row, probs_all, dscores_all, dq, dk, dv,
+    q_back, k_back, v_back, w_part, w_near, w_mid, w_far, sources,
     send, recv, a_send, a_recv, b_send, b_recv, pass_send, pass_recv,
     near_send, near_recv, far_send, far_recv,
     back_send, back_recv, half_send, half_recv, local,
@@ -241,21 +241,19 @@
             return g_own.at[head], g_all.at[at]
         return delta_own.at[head], d_all.at[at]
 
-    def outgoing(kind, step):
-        peer = lax.rem(me + step, count)
+    def outgoing(kind, peer):
         source, target = piece(kind, peer, me)
-        return remote(source, target, send.at[kind, step], recv.at[kind, me], (peer, core))
-
-    def incoming(kind, step):
-        peer = lax.rem(me + step, count)
+        return remote(source, target, send.at[kind, peer], recv.at[kind, me], (peer, core))
+
+    def incoming(kind, peer):
         source, target = piece(kind, me, peer)
-        return remote(source, target, send.at[kind, step], recv.at[kind, peer], (peer, core))
+        return remote(source, target, send.at[kind, peer], recv.at[kind, peer], (peer, core))
 
     def await_pieces(kinds):
-        @pl.loop(1, count)
-        def _(step):
+        @pl.loop(0, count - 1)
+        def _(turn):
             for kind in kinds:
-                incoming(kind, step).wait_recv()
+                incoming(kind, peer_at(turn)).wait_recv()
 
     def a_piece(part, to_column, slot):
         return (
@@ -314,9 +312,13 @@
     def plane_peer(step):
         return lax.rem(column + step, side)
 
-    def far_first(turn):
-        far = count - side
-        return jnp.where(turn < far, turn + side, lax.rem(turn - far + 1, side))
+    upward = jnp.where(row < near_side, 1, side - 1)
+
+    def peer_at(turn):
+        far = turn < count - side
+        next_row = lax.rem(row + (turn // side + 1) * upward, side)
+        shift = jnp.where(far, lax.rem(turn, side), turn - (count - side) + 1)
+        return jnp.where(far, next_row, row) * side + lax.rem(column + shift, side)
 
     def near_peer(step):
         return near_base + lax.rem(near_at + step, near_side)
@@ -348,22 +350,18 @@
     def start_returns(kinds):
         @pl.loop(0, count - 1)
         def _(turn):
-            step = far_first(turn)
-            peer = lax.rem(me + step, count)
+            peer = peer_at(turn)
             for at in kinds:
-                back_copy(at, peer, me, step, me, (peer, core)).start()
+                back_copy(at, peer, me, peer, me, (peer, core)).start()
 
         for at in kinds:
             source, target = backs[at]
-            pltpu.make_async_copy(
-                source.at[me], target.at[:, head_cut(me)], local.at[at]
-            ).start()
+            target[:, head_cut(me)] = source[me]
 
     @pl.loop(0, count - 1)
     def _(turn):
-        step = far_first(turn)
         for kind in (0, 1):
-            outgoing(kind, step).start()
+            outgoing(kind, peer_at(turn)).start()
 
     for step in range(1, side):
         for part in range(side):
@@ -388,7 +386,7 @@
 
     @pl.loop(0, count - 1)
     def _(turn):
-        outgoing(3, far_first(turn)).start()
+        outgoing(3, peer_at(turn)).start()
 
     l_all[owner_blocks(me)] = log_own[me]
     for copy in loads[1:]:
@@ -399,7 +397,7 @@
 
     @pl.loop(0, count)
     def _(turn):
-        head = lax.rem(me + far_first(turn), count)
+        head = jnp.where(turn < count - 1, peer_at(turn), me)
         grads = lax.dot_general(
             b_own[...], w_own[head_cut(head), :], by_rows, preferred_element_type=jnp.float32
         ).astype(low)
@@ -415,16 +413,16 @@
 
         @pl.when(turn > 0)
         def _():
-            step = far_first(turn - 1)
             for kind in (4, 5):
-                outgoing(kind, step).start()
+                outgoing(kind, peer_at(turn - 1)).start()
 
     g_all[owner_blocks(me)] = g_own[me]
     d_all[owner_blocks(me)] = delta_own[me]
 
     @pl.loop(0, count - 1)
     def _(turn):
-        outgoing(2, far_first(turn)).start()
+        outgoing(2, peer_at(turn)).start()
+
 
     for group in range(groups):
         for step, turn in b_routes:
@@ -559,32 +557,39 @@
             at = pl.ds((sequence * side + slot) * rows, rows)
             a_turned[:, at] = a_all[sequence, slot].T
 
+    weight_stage(0)
     await_pieces((2,))
     in_order(((v_all, v_row),))
 
     @pl.loop(0, pairs)
     def _(at):
         i, j = pair_of(at)
-        q_tile, k_tile = q_row[cut(i), :], k_row[cut(j), :]
         dprobs = lax.dot_general(
             v_row[cut(j), :], g_row[cut(i), :], by_rows, preferred_element_type=jnp.float32
         )
         dscores = (probs_all[at] * (dprobs - line(d_row, i))).astype(low)
-        add_blocks(dk, j, jnp.dot(dscores, q_tile, preferred_element_type=jnp.float32))
-        add_blocks(
-            dq, i,
-            lax.dot_general(dscores, k_tile, by_columns, preferred_element_type=jnp.float32),
-        )
+        dscores_all[at] = dscores
+        add_blocks(dk, j, jnp.dot(dscores, q_row[cut(i), :], preferred_element_type=jnp.float32))
 
     for block in range(blocks):
         target = pl.ds(block % 2 * block_rows, block_rows)
         k_back[block // 2, target, :] = (dk[places[0, block]] * scaling).astype(low)
     start_returns((1,))
+    weight_stage(1)
+
+    @pl.loop(0, pairs)
+    def _(at):
+        i, j = pair_of(at)
+        add_blocks(
+            dq, i,
+            lax.dot_general(
+                dscores_all[at], k_row[cut(j), :], by_columns, preferred_element_type=jnp.float32
+            ),
+        )
+
     for block in range(blocks):
         target = pl.ds(block % 2 * block_rows, block_rows)
         q_back[block // 2, target, :] = (dq[places[0, block]] * scaling).astype(low)
-    weight_stage(0)
-    weight_stage(1)
     start_returns((0,))
     cross_stage(0)
     cross_stage(1)
@@ -599,13 +604,16 @@
         for step, turn in b_routes:
             b_outgoing(group, step, turn).wait_send()
 
-    @pl.loop(1, count)
-    def _(step):
+    @pl.loop(0, count - 1)
+    def _(turn):
         for kind in range(6):
-            outgoing(kind, step).wait_send()
+            outgoing(kind, peer_at(turn)).wait_send()
+
+    def half_cut(group, slot):
+        return pl.ds(pl.multiple_of((slot * groups + group) * sub, sub), sub)
 
     def half_copy(group, slot, turn, other):
-        block = w_half.at[group, slot]
+        block = w_out.at[:, half_cut(group, slot)]
         return remote(
             block, block, half_send.at[group, turn], half_recv.at[group, slot], (me, other)
         )
@@ -614,7 +622,7 @@
         far_copy(group).wait_send()
         far_copy(group).wait_recv()
         total = near_sum(group, row, 0) + w_far[group].astype(jnp.float32)
-        w_half[group, core] = total.astype(low)
+        w_out[:, half_cut(group, core)] = total.astype(low)
         for turn in range(1, cores):
             half_copy(group, core, turn, lax.rem(core + turn, cores)).start()
     for group in range(groups):
@@ -622,18 +630,13 @@
             other = lax.rem(core + turn, cores)
             half_copy(group, core, turn, other).wait_send()
             half_copy(group, other, turn, other).wait_recv()
-        for slot in range(cores):
-            w_out[:, pl.ds((slot * groups + group) * sub, sub)] = w_half[group, slot]
-
-    for at, (source, target) in enumerate(backs):
-        pltpu.make_async_copy(source.at[me], target.at[:, head_cut(me)], local.at[at]).wait()
-
-    @pl.loop(1, count)
-    def _(step):
-        peer = lax.rem(me + step, count)
+
+    @pl.loop(0, count - 1)
+    def _(turn):
+        peer = peer_at(turn)
         for at in range(3):
-            back_copy(at, peer, me, step, me, (peer, core)).wait_send()
-            back_copy(at, me, peer, step, peer, (peer, core)).wait_recv()
+            back_copy(at, peer, me, peer, me, (peer, core)).wait_send()
+            back_copy(at, me, peer, peer, peer, (peer, core)).wait_recv()
 
 
 def head_per_device(
@@ -664,10 +667,9 @@
     own_lines = (count, 2, 1, rows)
     grad_queries, grad_keys, grad_values, weight_share = pl.pallas_call(
         functools.partial(fused_kernel, count, side, cores, dim, tile, scaling),
-        out_shape=[jax.ShapeDtypeStruct((rows, width), low)] * 3
-        + [jax.ShapeDtypeStruct((dim, out_width), low)],
+        out_shape=[pltpu.VMEM((rows, width), low)] * 3 + [pltpu.VMEM((dim, out_width), low)],
         in_specs=[pl.BlockSpec(memory_space=pltpu.SMEM)] + [ANY] * 7,
-        out_specs=[ANY] * 3 + [vmem],
+        out_specs=[vmem] * 4,
         scratch_shapes=[pltpu.VMEM(block_shape, low)] * 4
         + [pltpu.VMEM(lines, jnp.float32)] * 2
         + [
@@ -683,13 +685,12 @@
         + [pltpu.VMEM(own_lines, jnp.float32)] * 2
         + [pltpu.VMEM(wide, low)] * 4
         + [pltpu.VMEM((count, 1, rows), jnp.float32)] * 2
-        + [pltpu.VMEM((tiles * (tiles + 1) // 2, tile, tile), jnp.float32)]
+        + [pltpu.VMEM((tiles * (tiles + 1) // 2, tile, tile), kind) for kind in (jnp.float32, low)]
         + [pltpu.VMEM(block_shape, jnp.float32)] * 3
         + [pltpu.VMEM(split, low)] * 3
         + [pltpu.VMEM((groups, side, dim, sub), low)]
         + [pltpu.VMEM((groups, near_side, 2, dim, sub), low)]
         + [pltpu.VMEM((groups, dim, sub), low)] * 2
-        + [pltpu.VMEM((groups, cores, dim, sub), low)]
         + [pltpu.SMEM((2 * count,), jnp.int32)]
         + [
             dma((6, count)), dma((6, count)),
@@ -702,7 +703,7 @@
             dma((groups, cores)), dma((groups, cores)), dma((side + groups + 7,)),
         ],
         compiler_params=pltpu.CompilerParams(
-            collective_id=0, has_side_effects=True, vmem_limit_bytes=60 * 1024 * 1024
+            collective_id=0, has_side_effects=True, vmem_limit_bytes=56 * 1024 * 1024
         ),
     )(
         block_pos,
@@ -710,19 +711,37 @@
         attn_out[0], grad_out[0], log_sums[0],
         out_weight,
     )
+    results = [
+        pltpu.with_memory_space_constraint(part, pltpu.VMEM)
+        for part in (grad_queries, grad_keys, grad_values, weight_share)
+    ]
     grad_queries, grad_keys, grad_values, weight_share = pl.pallas_call(
         leave_kernel,
         out_shape=[jax.ShapeDtypeStruct((rows, width), low)] * 3
         + [jax.ShapeDtypeStruct((dim, out_width), jnp.float32)],
         in_specs=[vmem] * 4,
-        out_specs=[vmem] * 4,
-    )(grad_queries, grad_keys, grad_values, weight_share)
+        out_specs=[ANY] * 4,
+        scratch_shapes=[
+            pltpu.VMEM((dim, out_width), jnp.float32), pltpu.SemaphoreType.DMA((4,)),
+        ],
+        compiler_params=pltpu.CompilerParams(vmem_limit_bytes=4 * 1024 * 1024),
+    )(*results)
     return grad_queries[None], grad_keys[None], grad_values[None], weight_share
 
 
-def leave_kernel(q_in, k_in, v_in, w_in, q_out, k_out, v_out, w_out):
-    for source, target in ((q_in, q_out), (k_in, k_out), (v_in, v_out), (w_in, w_out)):
-        target[...] = source[...].astype(target.dtype)
+def leave_kernel(q_in, k_in, v_in, w_in, q_out, k_out, v_out, w_out, w_wide, sems):
+    copies = [
+        pltpu.make_async_copy(source, target, sems.at[at])
+        for at, (source, target) in enumerate(
+            ((q_in, q_out), (k_in, k_out), (v_in, v_out), (w_wide, w_out))
+        )
+    ]
+    for copy in copies[:3]:
+        copy.start()
+    w_wide[...] = w_in[...].astype(w_wide.dtype)
+    copies[3].start()
+    for copy in copies:
+        copy.wait()
 
 
 def make_per_device(mesh):

time: 110 us -> 105 us (0.955)
  the two profiles are of different devices: /device:TPU:0 before, /device:TPU:16 now
where the time goes in v2:
time: 105 us; the launch traced here: 104 us
  Pallas kernels  103 us (98%)
    pallas_call x1, Pallas kernels, head_per_device(): pl.pallas_call(functools.partial(fused_kernel, count, side, cores, dim, t...  102 us

profile of v2, /device:TPU:16, one launch (start us, length us, event | category | flops | bytes accessed | tf_op | source)
XLA Modules:
  0.0 104.1 jit_solution(8100352198969204416)
XLA Ops:
  0.6 102.0 %shard_map.111 = (bf16[128,2048]{1,0:T(8,128)(2,1)S(1)}, bf16[128,2048]{1,0:T(8,128)(2,1)S(1)}, bf16[128,2048]{1,0:T(8,128)(2,1)S(1)}, bf16[128,2048]{1,0:T(8,128)(2,1)S(1)}) custom-call(s32[1,32]{1,0:T(1,128)} %places.1, bf16[2,64,2048]{2,1,0:T(8,128)(2,1)} %bitcast.9, bf16[2,64,2048]{2,1,0:T(8,128)(2,1)} %bitcast.10, bf16[2,64,2048]{2,1,0:T(8,128)(2,1)} %bitcast.11, ...), custom_call_target="tpu_custom_call" | custom-call | tf_op jit(solution)/shard_map/pallas_call | solution.py:668
  102.6 1.5 %shard_map.112 = (bf16[128,2048]{1,0:T(8,128)(2,1)}, bf16[128,2048]{1,0:T(8,128)(2,1)}, bf16[128,2048]{1,0:T(8,128)(2,1)}, f32[128,2048]{1,0:T(8,128)}) custom-call(bf16[128,2048]{1,0:T(8,128)(2,1)S(1)} %get-tuple-element.12.q_in, bf16[128,2048]{1,0:T(8,128)(2,1)S(1)} %get-tuple-element.13.k_in, bf16[128,2048]{1,0:T(8,128)(2,1)S(1)} %get-tuple-element.14.v_in, ...), custom_call_target="tpu_custom_call" | custom-call | tf_op jit(solution)/shard_map/pallas_call | solution.py:718

commit v3 on v2

--- a/solution.py
+++ b/solution.py
@@ -182,8 +182,8 @@
     places, q_in, k_in, v_in, a_in, b_in, l_in, w_in,
     q_out, k_out, v_out, w_out,
     q_all, k_all, v_all, g_all, l_all, d_all, a_all, b_all, a_turned,
-    a_own, b_own, l_own, w_own, g_own, log_own, delta_own,
-    q_row, k_row, v_row, g_row, l_row, d_row, probs_all, dscores_all, dq, dk, dv,
+    q_own, k_own, a_own, b_own, l_own, w_own, g_own, log_own, delta_own,
+    q_row, k_row, v_row, g_row, l_block, d_block, l_row, d_row, probs_all, dscores_all, dq, dk, dv,
     q_back, k_back, v_back, w_part, w_near, w_mid, w_far, sources,
     send, recv, a_send, a_recv, b_send, b_recv, pass_send, pass_recv,
     near_send, near_recv, far_send, far_recv,
@@ -204,7 +204,10 @@
     loads = [
         pltpu.make_async_copy(source, target, local.at[at])
         for at, (source, target) in enumerate(
-            [(l_in, l_own), (b_in, b_own), (w_in, w_own), (a_in, a_own)]
+            [
+                (q_in, q_own), (k_in, k_own),
+                (l_in, l_own), (b_in, b_own), (w_in, w_own), (a_in, a_own),
+            ]
         )
     ]
     for copy in loads:
@@ -230,16 +233,16 @@
         cut = head_cut(head)
         at = owner_blocks(owner)
         if kind == 0:
-            return q_in.at[:, :, cut], q_all.at[at]
+            return q_own.at[:, :, cut], q_all.at[at]
         if kind == 1:
-            return k_in.at[:, :, cut], k_all.at[at]
+            return k_own.at[:, :, cut], k_all.at[at]
         if kind == 2:
             return v_in.at[:, :, cut], v_all.at[at]
         if kind == 3:
-            return log_own.at[head], l_all.at[at]
+            return log_own.at[head], l_all.at[owner]
         if kind == 4:
             return g_own.at[head], g_all.at[at]
-        return delta_own.at[head], d_all.at[at]
+        return delta_own.at[head], d_all.at[owner]
 
     def outgoing(kind, peer):
         source, target = piece(kind, peer, me)
@@ -347,16 +350,20 @@
             back_send.at[at, out_index], back_recv.at[at, in_index], device,
         )
 
-    def start_returns(kinds):
-        @pl.loop(0, count - 1)
+    def start_returns(kinds, first=0, last=count - 1):
+        @pl.loop(first, last)
         def _(turn):
             peer = peer_at(turn)
             for at in kinds:
                 back_copy(at, peer, me, peer, me, (peer, core)).start()
 
-        for at in kinds:
-            source, target = backs[at]
-            target[:, head_cut(me)] = source[me]
+        if last == count - 1:
+            for at in kinds:
+                source, target = backs[at]
+                target[:, head_cut(me)] = source[me]
+
+    for copy in loads[:2]:
+        copy.wait()
 
     @pl.loop(0, count - 1)
     def _(turn):
@@ -367,29 +374,28 @@
         for part in range(side):
             a_outgoing(part, step).start()
     owns = [
-        pltpu.make_async_copy(source, target, local.at[4 + at])
+        pltpu.make_async_copy(source, target, local.at[6 + at])
         for at, (source, target) in enumerate(
             [a_piece(part, column, column) for part in range(side)]
             + [b_piece(group, core, core, column) for group in range(groups)]
-            + [piece(kind, me, me) for kind in range(3)]
+            + [piece(2, me, me)]
         )
     ]
     for copy in owns:
         copy.start()
-    loads[0].wait()
+    loads[2].wait()
     early_half = lax.broadcasted_iota(jnp.int32, (1, rows), 1) < block_rows
     for head in range(count):
-        logs = l_own[head : head + 1, :]
-        turned = pltpu.roll(logs, block_rows, 1)
-        log_own[head, 0] = jnp.where(early_half, logs, turned)
-        log_own[head, 1] = jnp.where(early_half, turned, logs)
+        log_own[head] = l_own[head : head + 1, :]
 
     @pl.loop(0, count - 1)
     def _(turn):
         outgoing(3, peer_at(turn)).start()
 
-    l_all[owner_blocks(me)] = log_own[me]
-    for copy in loads[1:]:
+    q_all[owner_blocks(me)] = q_own[:, :, head_cut(me)]
+    k_all[owner_blocks(me)] = k_own[:, :, head_cut(me)]
+    l_all[me] = log_own[me]
+    for copy in loads[3:]:
         copy.wait()
 
     by_rows = (((1,), (1,)), ((), ()))
@@ -406,10 +412,8 @@
         deltas = lax.dot_general(
             jnp.ones((8, dim), jnp.float32), product, by_rows,
             precision=lax.Precision.HIGHEST, preferred_element_type=jnp.float32,
-        )[0:1]
-        turned = pltpu.roll(deltas, block_rows, 1)
-        delta_own[head, 0] = jnp.where(early_half, deltas, turned)
-        delta_own[head, 1] = jnp.where(early_half, turned, deltas)
+        )
+        delta_own[head] = deltas[0:1]
 
         @pl.when(turn > 0)
         def _():
@@ -417,7 +421,7 @@
                 outgoing(kind, peer_at(turn - 1)).start()
 
     g_all[owner_blocks(me)] = g_own[me]
-    d_all[owner_blocks(me)] = delta_own[me]
+    d_all[me] = delta_own[me]
 
     @pl.loop(0, count - 1)
     def _(turn):
@@ -443,7 +447,12 @@
             for raw, ordered in pairs:
                 ordered[pl.ds(place * block_rows, block_rows), :] = raw[block]
 
-    def in_order_lines(raw, ordered):
+    def in_order_lines(received, raw, ordered):
+        for owner in range(count):
+            values = received[owner]
+            turned = pltpu.roll(values, block_rows, 1)
+            raw[2 * owner] = jnp.where(early_half, values, turned)
+            raw[2 * owner + 1] = jnp.where(early_half, turned, values)
         for pair_at in range(blocks // 2):
             early = raw[sources[2 * pair_at]]
             late = raw[sources[2 * pair_at + 1]]
@@ -469,7 +478,7 @@
 
     await_pieces((0, 1, 3))
     in_order(((q_all, q_row), (k_all, k_row)))
-    in_order_lines(l_all, l_row)
+    in_order_lines(l_all, l_block, l_row)
 
     @pl.loop(0, pairs)
     def _(at):
@@ -528,7 +537,7 @@
 
     await_pieces((4, 5))
     in_order(((g_all, g_row),))
-    in_order_lines(d_all, d_row)
+    in_order_lines(d_all, d_block, d_row)
     dv[...] = jnp.zeros_like(dv)
     dk[...] = jnp.zeros_like(dk)
     dq[...] = jnp.zeros_like(dq)
@@ -664,18 +673,20 @@
     block_shape = (2 * count, block_rows, dim)
     split = (count, rows, dim)
     lines = (2 * count, 1, rows)
-    own_lines = (count, 2, 1, rows)
+    own_lines = (count, 1, rows)
     grad_queries, grad_keys, grad_values, weight_share = pl.pallas_call(
         functools.partial(fused_kernel, count, side, cores, dim, tile, scaling),
         out_shape=[pltpu.VMEM((rows, width), low)] * 3 + [pltpu.VMEM((dim, out_width), low)],
         in_specs=[pl.BlockSpec(memory_space=pltpu.SMEM)] + [ANY] * 7,
         out_specs=[vmem] * 4,
         scratch_shapes=[pltpu.VMEM(block_shape, low)] * 4
-        + [pltpu.VMEM(lines, jnp.float32)] * 2
+        + [pltpu.VMEM(own_lines, jnp.float32)] * 2
         + [
             pltpu.VMEM((cores, side, rows, side * dim), low),
             pltpu.VMEM((cores, side, rows, share), low),
             pltpu.VMEM((side * dim, cores * side * rows), low),
+            pltpu.VMEM((2, block_rows, width), low),
+            pltpu.VMEM((2, block_rows, width), low),
             pltpu.VMEM((rows, width), low),
             pltpu.VMEM((rows, out_width), low),
             pltpu.VMEM((heads, rows), jnp.float32),
@@ -684,7 +695,8 @@
         ]
         + [pltpu.VMEM(own_lines, jnp.float32)] * 2
         + [pltpu.VMEM(wide, low)] * 4
-        + [pltpu.VMEM((count, 1, rows), jnp.float32)] * 2
+        + [pltpu.VMEM(lines, jnp.float32)] * 2
+        + [pltpu.VMEM(own_lines, jnp.float32)] * 2
         + [pltpu.VMEM((tiles * (tiles + 1) // 2, tile, tile), kind) for kind in (jnp.float32, low)]
         + [pltpu.VMEM(block_shape, jnp.float32)] * 3
         + [pltpu.VMEM(split, low)] * 3

time: 105 us -> 104 us (level)
  no operation moved by 1% of the time
where the time goes in v3:
time: 104 us
  Pallas kernels  103 us (99%)
    pallas_call x1, Pallas kernels, head_per_device(): pl.pallas_call(functools.partial(fused_kernel, count, side, cores, dim, t...  101 us

profile of v3, /device:TPU:16, one launch (start us, length us, event | category | flops | bytes accessed | tf_op | source)
XLA Modules:
  0.0 103.6 jit_solution(6713430639180783515)
XLA Ops:
  0.6 101.4 %shard_map.111 = (bf16[128,2048]{1,0:T(8,128)(2,1)S(1)}, bf16[128,2048]{1,0:T(8,128)(2,1)S(1)}, bf16[128,2048]{1,0:T(8,128)(2,1)S(1)}, bf16[128,2048]{1,0:T(8,128)(2,1)S(1)}) custom-call(s32[1,32]{1,0:T(1,128)} %places.1, bf16[2,64,2048]{2,1,0:T(8,128)(2,1)} %bitcast.9, bf16[2,64,2048]{2,1,0:T(8,128)(2,1)} %bitcast.10, bf16[2,64,2048]{2,1,0:T(8,128)(2,1)} %bitcast.11, ...), custom_call_target="tpu_custom_call" | custom-call | tf_op jit(solution)/shard_map/pallas_call | solution.py:677
  102.0 1.5 %shard_map.112 = (bf16[128,2048]{1,0:T(8,128)(2,1)}, bf16[128,2048]{1,0:T(8,128)(2,1)}, bf16[128,2048]{1,0:T(8,128)(2,1)}, f32[128,2048]{1,0:T(8,128)}) custom-call(bf16[128,2048]{1,0:T(8,128)(2,1)S(1)} %get-tuple-element.12.q_in, bf16[128,2048]{1,0:T(8,128)(2,1)S(1)} %get-tuple-element.13.k_in, bf16[128,2048]{1,0:T(8,128)(2,1)S(1)} %get-tuple-element.14.v_in, ...), custom_call_target="tpu_custom_call" | custom-call | tf_op jit(solution)/shard_map/pallas_call | solution.py:730

commit v4 on v3

--- a/solution.py
+++ b/solution.py
@@ -599,9 +599,10 @@
     for block in range(blocks):
         target = pl.ds(block % 2 * block_rows, block_rows)
         q_back[block // 2, target, :] = (dq[places[0, block]] * scaling).astype(low)
-    start_returns((0,))
+    start_returns((0,), 0, count // 2)
     cross_stage(0)
     cross_stage(1)
+    start_returns((0,), count // 2)
 
     for step in range(1, side):
         for part in range(side):

time: 104 us -> 104 us (level)
  no operation moved by 1% of the time
where the time goes in v4:
time: 104 us
  Pallas kernels  103 us (99%)
    pallas_call x1, Pallas kernels, head_per_device(): pl.pallas_call(functools.partial(fused_kernel, count, side, cores, dim, t...  101 us

profile of v4, /device:TPU:16, one launch (start us, length us, event | category | flops | bytes accessed | tf_op | source)
XLA Modules:
  0.0 103.6 jit_solution(2383923300486082637)
XLA Ops:
  0.6 101.4 %shard_map.111 = (bf16[128,2048]{1,0:T(8,128)(2,1)S(1)}, bf16[128,2048]{1,0:T(8,128)(2,1)S(1)}, bf16[128,2048]{1,0:T(8,128)(2,1)S(1)}, bf16[128,2048]{1,0:T(8,128)(2,1)S(1)}) custom-call(s32[1,32]{1,0:T(1,128)} %places.1, bf16[2,64,2048]{2,1,0:T(8,128)(2,1)} %bitcast.9, bf16[2,64,2048]{2,1,0:T(8,128)(2,1)} %bitcast.10, bf16[2,64,2048]{2,1,0:T(8,128)(2,1)} %bitcast.11, ...), custom_call_target="tpu_custom_call" | custom-call | tf_op jit(solution)/shard_map/pallas_call | solution.py:678
  102.0 1.5 %shard_map.112 = (bf16[128,2048]{1,0:T(8,128)(2,1)}, bf16[128,2048]{1,0:T(8,128)(2,1)}, bf16[128,2048]{1,0:T(8,128)(2,1)}, f32[128,2048]{1,0:T(8,128)}) custom-call(bf16[128,2048]{1,0:T(8,128)(2,1)S(1)} %get-tuple-element.12.q_in, bf16[128,2048]{1,0:T(8,128)(2,1)S(1)} %get-tuple-element.13.k_in, bf16[128,2048]{1,0:T(8,128)(2,1)S(1)} %get-tuple-element.14.v_in, ...), custom_call_target="tpu_custom_call" | custom-call | tf_op jit(solution)/shard_map/pallas_call | solution.py:731
